TPU v7x, 32 devices: a whole 2x2x4 slice. The times are simulated.
32 devices in a mesh: scan: 4 (over y, core), ascan: 8 (over z, x).
Axes of the slice: x: 2, y: 2, z: 4, core: 2. Of those that a mesh axis runs over, the one named last changes fastest.
Arguments:
- spectra: bfloat16 [8, 4, 1024, 2048], P('scan', None, 'ascan'), may hold values from -8 to 8
- surface_top: int32 [8, 1024], P('scan', 'ascan'), may hold values from 0 to 3, as said below
- surface_bottom: int32 [8, 1024], P('scan', 'ascan'), may hold values from 1 to 8, as said below
Outputs:
- angiogram: float32 [8, 1024, 1024], P('scan', 'ascan')
- structure_map: float32 [8, 1024, 1024], P('scan', 'ascan')
- speckle_map: float32 [8, 1024, 1024], P('scan', 'ascan')
- mean_flow: float32 [], replicated
Inputs may be any that keep to these rules, and one draw needn't show every extreme that they name: surface_top counts tiles of 128 depth rows. surface_bottom is greater than surface_top of the same A-scan.
All inputs are finite; a program needn't handle non-finite values.
Results may differ from a plain program's by a relative error of at most 0.0032.
Values sent between devices are 32-bit elements; how exact they have to be, the bound alone decides.
No kernel may reach another device: no remote copies, remote signals or barrier semaphores. Data moves between devices by JAX's collectives and lax.ppermute only.
A program may use at most 128 MiB of HBM per device.

v0:
```python
import math
import jax
import jax.numpy as jnp
from jax import lax
from jax.sharding import PartitionSpec as P

REPEATS = 4
BINS = 2048
BANDS = 4
TILE = 128
BAND_BINS = 512
DEPTH = 1024
FLOOR_SHARE = 0.05
VARIANCE_SCALE = 0.1


def make_table():
    sample = jnp.arange(BAND_BINS, dtype=jnp.int32)
    depth_index = jnp.arange(DEPTH, dtype=jnp.int32)
    product = sample[:, None] * depth_index[None, :] % BINS
    phase_angle = product.astype(jnp.float32) * (2.0 * math.pi / BINS)
    window = jnp.sin(math.pi * (sample.astype(jnp.float32) + 0.5) / BAND_BINS) ** 2
    cosine = window[:, None] * jnp.cos(phase_angle)
    sine = window[:, None] * jnp.sin(phase_angle)
    return jnp.concatenate([cosine, sine], axis=1).astype(jnp.bfloat16)


def band_moments(spectra, table_part, surface_top, surface_bottom):
    scan_count, repeat_count, ascan_count, bin_count = spectra.shape
    depth_width = table_part.shape[1] // 2
    flat = spectra.reshape(scan_count * repeat_count * ascan_count, BANDS, BAND_BINS)
    similarity_total = jnp.zeros((scan_count, ascan_count, depth_width), jnp.float32)
    amplitude_total = jnp.zeros((scan_count, ascan_count, depth_width), jnp.float32)
    variance_total = jnp.zeros((scan_count, ascan_count, depth_width), jnp.float32)
    for band_index in range(BANDS):
        profile = jnp.dot(flat[:, band_index, :], table_part, preferred_element_type=jnp.float32)
        profile = profile.reshape(scan_count, repeat_count, ascan_count, 2 * depth_width)
        amplitude = jnp.sqrt(profile[..., :depth_width] ** 2 + profile[..., depth_width:] ** 2)
        earlier = amplitude[:, :-1]
        later = amplitude[:, 1:]
        similarity = (
            2.0 * earlier * later / jnp.maximum(earlier**2 + later**2, FLOOR_SHARE * BAND_BINS)
        )
        similarity_total = similarity_total + jnp.sum(similarity, axis=1)
        amplitude_total = amplitude_total + jnp.sum(amplitude, axis=1)
        repeat_mean = jnp.mean(amplitude, axis=1, keepdims=True)
        variance_total = variance_total + jnp.mean((amplitude - repeat_mean) ** 2, axis=1)
    depth_rows = jnp.arange(depth_width, dtype=jnp.int32)
    lower = depth_rows[None, None, :] >= surface_top[..., None] * TILE
    upper = depth_rows[None, None, :] < surface_bottom[..., None] * TILE
    inside = (lower & upper).astype(jnp.float32)
    decorrelation = (1.0 - similarity_total / (BANDS * (REPEATS - 1))) * inside
    structure = amplitude_total / (BANDS * REPEATS) / math.sqrt(BAND_BINS) * inside
    speckle = variance_total / BANDS / (VARIANCE_SCALE * BAND_BINS) * inside
    return (decorrelation, structure, speckle, jnp.sum(decorrelation), jnp.sum(inside))


def body(spectra, surface_top, surface_bottom):
    dft_table = make_table()
    decorrelation, structure, speckle, flow_sum, tissue_count = band_moments(
        spectra, dft_table, surface_top, surface_bottom
    )
    totals = lax.psum((flow_sum, tissue_count), ("scan", "ascan"))
    mean_flow = totals[0] / totals[1]
    decorrelation, structure, speckle = (
        lax.all_to_all(decorrelation, "ascan", split_axis=2, concat_axis=1, tiled=True),
        lax.all_to_all(structure, "ascan", split_axis=2, concat_axis=1, tiled=True),
        lax.all_to_all(speckle, "ascan", split_axis=2, concat_axis=1, tiled=True),
    )
    padded = jnp.pad(decorrelation, ((0, 0), (1, 1), (0, 0)))
    smoothed = (padded[:, :-2] + padded[:, 1:-1] + padded[:, 2:]) / 3.0
    angiogram = jnp.swapaxes(smoothed / mean_flow, 1, 2)
    return (angiogram, jnp.swapaxes(structure, 1, 2), jnp.swapaxes(speckle, 1, 2), mean_flow)


def solution(mesh):
    return jax.shard_map(
        body,
        mesh=mesh,
        in_specs=(P("scan", None, "ascan", None), P("scan", "ascan"), P("scan", "ascan")),
        out_specs=(
            P("scan", "ascan", None),
            P("scan", "ascan", None),
            P("scan", "ascan", None),
            P(),
        ),
        check_vma=False,
    )
```

profile of v0, /device:TPU:0, one launch (start us, length us, event | category | flops | bytes accessed | tf_op | source)
XLA Modules:
  0.0 194.1 jit_solution(11013518984003762521)
XLA Ops:
  0.7 7.8 %reshape.51 = bf16[1024,4,512]{2,1,0:T(4,128)(2,1)} reshape(bf16[2,4,128,2048]{3,2,1,0:T(8,128)(2,1)} %param.3) | data formatting | bytes 8388608 | tf_op jit(solution)/shard_map/reshape | solution.py:31
  8.5 13.4 %fusion.36 = (bf16[1024,1,512]{2,1,0:T(2,128)(2,1)S(1)}, bf16[1024,1,512]{2,1,0:T(2,128)(2,1)S(1)}, bf16[1024,1,512]{2,1,0:T(2,128)(2,1)S(1)}, bf16[1024,1,512]{2,1,0:T(2,128)(2,1)S(1)}) fusion(bf16[1024,4,512]{2,1,0:T(4,128)(2,1)} %reshape.51), kind=kLoop, calls=%fused_computation.68 | loop fusion | bytes 8388608 | tf_op jit(solution)/shard_map/slice | solution.py:36
  22.0 8.7 %multiply_convert_fusion.1 = (bf16[512,1024]{1,0:T(8,128)(2,1)S(1)}, bf16[512,1024]{1,0:T(8,128)(2,1)S(1)}) fusion(f32[512]{0:T(512)S(1)} %sine_multiply_fusion), kind=kLoop, calls=%fused_computation.32 | loop fusion | flops 9437184 | bytes 2099200 | tf_op jit(solution)/shard_map/convert
  30.6 2.4 %fusion.20 = f32[2048,1024]{0,1:T(8,128)S(1)} fusion(bf16[1024,1,512]{2,1,0:T(2,128)(2,1)S(1)} %get-tuple-element.24, bf16[512,1024]{1,0:T(8,128)(2,1)S(1)} %get-tuple-element.37, bf16[512,1024]{1,0:T(8,128)(2,1)S(1)} %get-tuple-element.36), kind=kOutput, calls=%fused_computation.42 | convolution fusion | flops 2151677952 | bytes 11534336 | tf_op jit(solution)/shard_map/dot_general | solution.py:36
  33.0 5.6 %fusion.23 = f32[2048,1024]{0,1:T(8,128)} fusion(bf16[1024,1,512]{2,1,0:T(2,128)(2,1)S(1)} %get-tuple-element.27, bf16[512,1024]{1,0:T(8,128)(2,1)S(1)} %get-tuple-element.37, bf16[512,1024]{1,0:T(8,128)(2,1)S(1)} %get-tuple-element.36), kind=kOutput, calls=%fused_computation.45 | convolution fusion | flops 2151677952 | bytes 11534336 | tf_op jit(solution)/shard_map/dot_general | solution.py:36
  38.6 2.3 %fusion.17 = f32[2048,1024]{0,1:T(8,128)S(1)} fusion(bf16[1024,1,512]{2,1,0:T(2,128)(2,1)S(1)} %get-tuple-element.26, bf16[512,1024]{1,0:T(8,128)(2,1)S(1)} %get-tuple-element.37, bf16[512,1024]{1,0:T(8,128)(2,1)S(1)} %get-tuple-element.36), kind=kOutput, calls=%fused_computation.39 | convolution fusion | flops 2151677952 | bytes 11534336 | tf_op jit(solution)/shard_map/dot_general | solution.py:36
  40.9 5.6 %fusion.14 = f32[2048,1024]{0,1:T(8,128)} fusion(bf16[1024,1,512]{2,1,0:T(2,128)(2,1)S(1)} %get-tuple-element.25, bf16[512,1024]{1,0:T(8,128)(2,1)S(1)} %get-tuple-element.37, bf16[512,1024]{1,0:T(8,128)(2,1)S(1)} %get-tuple-element.36), kind=kOutput, calls=%fused_computation.36 | convolution fusion | flops 2151677952 | bytes 11534336 | tf_op jit(solution)/shard_map/dot_general | solution.py:36
  46.5 6.6 %fusion.31 = (f32[2,128,1024]{2,1,0:T(8,128)S(1)}, f32[2,4,128,1024]{3,2,1,0:T(8,128)S(1)}, f32[2,128,1024]{2,1,0:T(8,128)}, f32[2,4,128,1024]{3,2,1,0:T(8,128)S(1)}) fusion(f32[2,4,128,2048]{3,2,1,0:T(8,128)S(1)} %bitcast.46, f32[2,4,128,2048]{3,2,1,0:T(8,128)} %bitcast.47), kind=kLoop, calls=%fused_computation.65 | loop fusion | flops 7864320 | bytes 27262976 | tf_op jit(solution)/shard_map/reduce_sum | solution.py:45
  56.0 5.5 %fusion.27 = (f32[2,128,1024]{2,1,0:T(8,128)S(1)}, f32[2,4,128,1024]{3,2,1,0:T(8,128)S(1)}, f32[2,128,1024]{2,1,0:T(8,128)S(1)}, f32[2,4,128,1024]{3,2,1,0:T(8,128)S(1)}) fusion(f32[2,4,128,2048]{3,2,1,0:T(8,128)S(1)} %bitcast.44, f32[2,4,128,2048]{3,2,1,0:T(8,128)} %bitcast.45), kind=kLoop, calls=%fused_computation.63 | loop fusion | flops 7864320 | bytes 27262976 | tf_op jit(solution)/shard_map/reduce_sum | solution.py:45
  65.5 3.6 %broadcast_multiply_fusion.2 = (f32[2,128,1024]{2,1,0:T(8,128)}, f32[2,128,1024]{2,1,0:T(8,128)S(1)}, f32[2,128,1024]{2,1,0:T(8,128)}, f32[2,128,1024]{2,1,0:T(8...) fusion(f32[2,128,1024]{2,1,0:T(8,128)S(1)} %get-tuple-element.14, ...), kind=kLoop, calls=%fused_computation.58 | loop fusion | flops 5505022 | bytes 14682120 | tf_op jit(solution)/shard_map/div | solution.py:46
  69.1 1.3 copy.21
  70.4 7.3 %all-to-all-start = ((f32[2,128,1024]{1,0,2:T(2,128)}), f32[2,128,1024]{1,0,2:T(2,128)S(1)}, u32[]{:S(2)}, u32[]{:S(2)}) async-start(f32[2,128,1024]{1,0,2:T(2,128)} %copy.21), calls=%async_computation | async-start | bytes 2097152 | tf_op jit(solution)/shard_map/all_to_all | solution.py:66
  79.0 24.5 %all-to-all-done = f32[2,128,1024]{1,0,2:T(2,128)S(1)} async-done(((f32[2,128,1024]{1,0,2:T(2,128)}), f32[2,128,1024]{1,0,2:T(2,128)S(1)}, u32[]{:S(2)}, u32[]{:S(2)}) %all-to-all-start) | async-done | bytes 1048608 | tf_op jit(solution)/shard_map/all_to_all | solution.py:66
  103.4 3.8 %all-to-all-start.1 = ((f32[2,128,1024]{1,0,2:T(2,128)}), f32[2,128,1024]{1,0,2:T(2,128)S(1)}, u32[]{:S(2)}, u32[]{:S(2)}) async-start(f32[2,128,1024]{1,0,2:T(2,128)} %copy.24), calls=%async_computation.1 | async-start | bytes 2097152 | tf_op jit(solution)/shard_map/all_to_all | solution.py:67
  107.2 3.4 %multiply_reduce_fusion = f32[2,128,1024]{2,1,0:T(8,128)S(1)} fusion(f32[2,4,128,1024]{3,2,1,0:T(8,128)} %copy-done.2, f32[2,128,1024]{2,1,0:T(8,128)} %get-tuple-element.32), kind=kLoop, calls=%fused_computation.16 | loop fusion | flops 2883584 | bytes 6291456 | tf_op jit(solution)/shard_map/reduce_sum | solution.py:47
  112.0 1.5 copy-done.6
  114.5 1.5 copy-done.4
  117.3 1.3 copy.27
  118.6 14.4 %all-to-all-done.1 = f32[2,128,1024]{1,0,2:T(2,128)S(1)} async-done(((f32[2,128,1024]{1,0,2:T(2,128)}), f32[2,128,1024]{1,0,2:T(2,128)S(1)}, u32[]{:S(2)}, u32[]{:S(2)}) %all-to-all-start.1) | async-done | bytes 1048608 | tf_op jit(solution)/shard_map/all_to_all | solution.py:67
  133.0 4.2 %all-to-all-start.2 = ((f32[2,128,1024]{1,0,2:T(2,128)}), f32[2,128,1024]{1,0,2:T(2,128)}, u32[]{:S(2)}, u32[]{:S(2)}) async-start(f32[2,128,1024]{1,0,2:T(2,128)} %copy.27), calls=%async_computation.2 | async-start | bytes 2097152 | tf_op jit(solution)/shard_map/all_to_all | solution.py:68
  137.3 45.5 %all-reduce.1 = (f32[]{:T(128)}, f32[]{:T(128)}) all-reduce(f32[]{:T(128)} %get-tuple-element.34, f32[]{:T(128)} %get-tuple-element.33), channel_id=1, replica_groups=mesh['scan'=4,'ascan'=8] {'scan','ascan'}, use_global_device_ids=true, to_apply=%region_5.6 | all-reduce | flops 2 | bytes 16 | tf_op jit(solution)/shard_map/psum | solution.py:63
  185.2 1.6 copy.23
  187.0 1.3 copy.30
  191.7 1.3 copy.32
  (43 shorter events, 16.4 us)
Async XLA Ops:
  53.1 2.0 %copy-start = (f32[2,4,128,1024]{3,2,1,0:T(8,128)}, f32[2,4,128,1024]{3,2,1,0:T(8,128)S(1)}, u32[]{:S(2)}) copy-start(f32[2,4,128,1024]{3,2,1,0:T(8,128)S(1)} %get-tuple-element.19) | copy-start | bytes 12582916
  53.1 8.4 %copy-start.2 = (f32[2,4,128,1024]{3,2,1,0:T(8,128)}, f32[2,4,128,1024]{3,2,1,0:T(8,128)S(1)}, u32[]{:S(2)}) copy-start(f32[2,4,128,1024]{3,2,1,0:T(8,128)S(1)} %get-tuple-element.41) | copy-start | bytes 12582916
  61.5 1.9 copy-start.3
  61.5 7.6 %copy-start.5 = (f32[2,4,128,1024]{3,2,1,0:T(8,128)}, f32[2,4,128,1024]{3,2,1,0:T(8,128)S(1)}, u32[]{:S(2)}) copy-start(f32[2,4,128,1024]{3,2,1,0:T(8,128)S(1)} %get-tuple-element.39) | copy-start | bytes 12582916
  63.4 0.9 copy-start.11
  63.4 0.9 copy-start.12
  63.4 2.1 %copy-start.10 = (f32[2,128,1024]{2,1,0:T(8,128)S(1)}, f32[2,128,1024]{2,1,0:T(8,128)}, u32[]{:S(2)}) copy-start(f32[2,128,1024]{2,1,0:T(8,128)} %get-tuple-element.40) | copy-start | bytes 3145732
  70.4 33.0 %all-to-all-start = ((f32[2,128,1024]{1,0,2:T(2,128)}), f32[2,128,1024]{1,0,2:T(2,128)S(1)}, u32[]{:S(2)}, u32[]{:S(2)}) async-start(f32[2,128,1024]{1,0,2:T(2,128)} %copy.21), calls=%async_computation | async-start | bytes 2097152 | tf_op jit(solution)/shard_map/all_to_all | solution.py:66
  103.4 29.6 %all-to-all-start.1 = ((f32[2,128,1024]{1,0,2:T(2,128)}), f32[2,128,1024]{1,0,2:T(2,128)S(1)}, u32[]{:S(2)}, u32[]{:S(2)}) async-start(f32[2,128,1024]{1,0,2:T(2,128)} %copy.24), calls=%async_computation.1 | async-start | bytes 2097152 | tf_op jit(solution)/shard_map/all_to_all | solution.py:67
  107.2 3.8 %copy-start.1 = (f32[2,4,128,1024]{3,2,1,0:T(8,128)S(1)}, f32[2,4,128,1024]{3,2,1,0:T(8,128)}, u32[]{:S(2)}) copy-start(f32[2,4,128,1024]{3,2,1,0:T(8,128)} %copy-done) | copy-start | bytes 12582916
  107.2 4.0 %copy-start.9 = (f32[2,128,1024]{2,1,0:T(8,128)S(1)}, f32[2,128,1024]{2,1,0:T(8,128)}, u32[]{:S(2)}) copy-start(f32[2,128,1024]{2,1,0:T(8,128)} %get-tuple-element.31) | copy-start | bytes 3145732
  111.3 2.2 %copy-start.6 = (f32[2,4,128,1024]{3,2,1,0:T(8,128)S(1)}, f32[2,4,128,1024]{3,2,1,0:T(8,128)}, u32[]{:S(2)}) copy-start(f32[2,4,128,1024]{3,2,1,0:T(8,128)} %copy-done.5) | copy-start | bytes 12582916
  111.3 2.5 %copy-start.8 = (f32[2,128,1024]{2,1,0:T(8,128)S(1)}, f32[2,128,1024]{2,1,0:T(8,128)}, u32[]{:S(2)}) copy-start(f32[2,128,1024]{2,1,0:T(8,128)} %get-tuple-element.30) | copy-start | bytes 3145732
  113.8 2.2 %copy-start.4 = (f32[2,4,128,1024]{3,2,1,0:T(8,128)S(1)}, f32[2,4,128,1024]{3,2,1,0:T(8,128)}, u32[]{:S(2)}) copy-start(f32[2,4,128,1024]{3,2,1,0:T(8,128)} %copy-done.3) | copy-start | bytes 12582916
  113.8 2.5 %copy-start.7 = (f32[2,128,1024]{2,1,0:T(8,128)S(1)}, f32[2,128,1024]{2,1,0:T(8,128)}, u32[]{:S(2)}) copy-start(f32[2,128,1024]{2,1,0:T(8,128)} %get-tuple-element.28) | copy-start | bytes 3145732
  133.0 57.0 %all-to-all-start.2 = ((f32[2,128,1024]{1,0,2:T(2,128)}), f32[2,128,1024]{1,0,2:T(2,128)}, u32[]{:S(2)}, u32[]{:S(2)}) async-start(f32[2,128,1024]{1,0,2:T(2,128)} %copy.27), calls=%async_computation.2 | async-start | bytes 2097152 | tf_op jit(solution)/shard_map/all_to_all | solution.py:68
where the time goes:
time: 195 us; the launch traced here: 194 us
  blocking collectives  45.5 us (23%)
  local copies, waits for them, and re-layouts  41.2 us (21%)
  waiting for transfers between devices  38.9 us (20%)
  other arithmetic  34.1 us (17%)
  matrix products  15.8 us (8%)
  starting transfers between devices  15.3 us (8%)
  between operations  3.32 us (2%)
    psum x1, blocking collectives, body(): totals = lax.psum((flow_sum, tissue_count), ('scan', 'ascan'))  45.5 us
    all_to_all x1, waiting for transfers between devices, body(): lax.all_to_all(decorrelation, 'ascan', split_axis=2, concat_axis=1, tiled...  24.5 us
    dot_general x4, matrix products, band_moments(): jnp.dot(flat[:, band_index, :], table_part, preferred_element_type=jnp.fl...  15.8 us
    all_to_all x1, waiting for transfers between devices, body(): lax.all_to_all(structure, 'ascan', split_axis=2, concat_axis=1, tiled=True)  14.4 us
    slice x1, local copies, waits for them, and re-layouts, band_moments(): flat[:, band_index, :]  13.4 us
    reduce_sum x2, other arithmetic, band_moments(): amplitude_total = amplitude_total + jnp.sum(amplitude, axis=1)  12.1 us
    unnamed x29, local copies, waits for them, and re-layouts  11.4 us
    another operation x1, other arithmetic  8.66 us
  transfers between devices with their start and end apart: 3, of which 2 were waited for; matrix products, arithmetic and copies ran while one was open for 7% of the time, Pallas kernels for 0%

commit v1 on v0

--- a/solution.py
+++ b/solution.py
@@ -60,7 +60,7 @@
     decorrelation, structure, speckle, flow_sum, tissue_count = band_moments(
         spectra, dft_table, surface_top, surface_bottom
     )
-    totals = lax.psum((flow_sum, tissue_count), ("scan", "ascan"))
+    totals = lax.psum(lax.psum((flow_sum, tissue_count), "scan"), "ascan")
     mean_flow = totals[0] / totals[1]
     decorrelation, structure, speckle = (
         lax.all_to_all(decorrelation, "ascan", split_axis=2, concat_axis=1, tiled=True),

time: 195 us -> 182 us (0.933)
  blocking collectives: 45.5 us -> 31.9 us
    psum x1 -> x2, blocking collectives: 45.5 us -> 31.9 us  [body(): totals = lax.psum(lax.psum((flow_sum, tissue_count), 'scan'), 'ascan')]
  transfers between devices with their start and end apart: 3 -> 3, of which waited for: 2 -> 2; matrix products, arithmetic and copies ran while one was open for 7% -> 8% of each run, Pallas kernels for 0% -> 0%
where the time goes in v1:
time: 182 us; the launch traced here: 181 us
  local copies, waits for them, and re-layouts  41.2 us (23%)
  waiting for transfers between devices  38.9 us (21%)
  other arithmetic  34.1 us (19%)
  blocking collectives  31.9 us (18%)
  matrix products  15.8 us (9%)
  starting transfers between devices  15.3 us (8%)
  between operations  3.32 us (2%)
    psum x2, blocking collectives, body(): totals = lax.psum(lax.psum((flow_sum, tissue_count), 'scan'), 'ascan')  31.9 us
    all_to_all x1, waiting for transfers between devices, body(): lax.all_to_all(decorrelation, 'ascan', split_axis=2, concat_axis=1, tiled...  24.5 us
    dot_general x4, matrix products, band_moments(): jnp.dot(flat[:, band_index, :], table_part, preferred_element_type=jnp.fl...  15.8 us
    all_to_all x1, waiting for transfers between devices, body(): lax.all_to_all(structure, 'ascan', split_axis=2, concat_axis=1, tiled=True)  14.4 us
    slice x1, local copies, waits for them, and re-layouts, band_moments(): flat[:, band_index, :]  13.4 us
    reduce_sum x2, other arithmetic, band_moments(): amplitude_total = amplitude_total + jnp.sum(amplitude, axis=1)  12.1 us
    unnamed x29, local copies, waits for them, and re-layouts  11.4 us
    another operation x1, other arithmetic  8.66 us
  transfers between devices with their start and end apart: 3, of which 2 were waited for; matrix products, arithmetic and copies ran while one was open for 8% of the time, Pallas kernels for 0%

profile of v1, /device:TPU:0, one launch (start us, length us, event | category | flops | bytes accessed | tf_op | source)
XLA Modules:
  0.0 180.5 jit_solution(8122350976483552745)
XLA Ops:
  0.7 7.8 %reshape.51 = bf16[1024,4,512]{2,1,0:T(4,128)(2,1)} reshape(bf16[2,4,128,2048]{3,2,1,0:T(8,128)(2,1)} %param.3) | data formatting | bytes 8388608 | tf_op jit(solution)/shard_map/reshape | solution.py:31
  8.5 13.4 %fusion.36 = (bf16[1024,1,512]{2,1,0:T(2,128)(2,1)S(1)}, bf16[1024,1,512]{2,1,0:T(2,128)(2,1)S(1)}, bf16[1024,1,512]{2,1,0:T(2,128)(2,1)S(1)}, bf16[1024,1,512]{2,1,0:T(2,128)(2,1)S(1)}) fusion(bf16[1024,4,512]{2,1,0:T(4,128)(2,1)} %reshape.51), kind=kLoop, calls=%fused_computation.68 | loop fusion | bytes 8388608 | tf_op jit(solution)/shard_map/slice | solution.py:36
  22.0 8.7 %multiply_convert_fusion.1 = (bf16[512,1024]{1,0:T(8,128)(2,1)S(1)}, bf16[512,1024]{1,0:T(8,128)(2,1)S(1)}) fusion(f32[512]{0:T(512)S(1)} %sine_multiply_fusion), kind=kLoop, calls=%fused_computation.32 | loop fusion | flops 9437184 | bytes 2099200 | tf_op jit(solution)/shard_map/convert
  30.6 2.4 %fusion.20 = f32[2048,1024]{0,1:T(8,128)S(1)} fusion(bf16[1024,1,512]{2,1,0:T(2,128)(2,1)S(1)} %get-tuple-element.26, bf16[512,1024]{1,0:T(8,128)(2,1)S(1)} %get-tuple-element.39, bf16[512,1024]{1,0:T(8,128)(2,1)S(1)} %get-tuple-element.38), kind=kOutput, calls=%fused_computation.42 | convolution fusion | flops 2151677952 | bytes 11534336 | tf_op jit(solution)/shard_map/dot_general | solution.py:36
  33.0 5.6 %fusion.23 = f32[2048,1024]{0,1:T(8,128)} fusion(bf16[1024,1,512]{2,1,0:T(2,128)(2,1)S(1)} %get-tuple-element.29, bf16[512,1024]{1,0:T(8,128)(2,1)S(1)} %get-tuple-element.39, bf16[512,1024]{1,0:T(8,128)(2,1)S(1)} %get-tuple-element.38), kind=kOutput, calls=%fused_computation.45 | convolution fusion | flops 2151677952 | bytes 11534336 | tf_op jit(solution)/shard_map/dot_general | solution.py:36
  38.6 2.3 %fusion.17 = f32[2048,1024]{0,1:T(8,128)S(1)} fusion(bf16[1024,1,512]{2,1,0:T(2,128)(2,1)S(1)} %get-tuple-element.28, bf16[512,1024]{1,0:T(8,128)(2,1)S(1)} %get-tuple-element.39, bf16[512,1024]{1,0:T(8,128)(2,1)S(1)} %get-tuple-element.38), kind=kOutput, calls=%fused_computation.39 | convolution fusion | flops 2151677952 | bytes 11534336 | tf_op jit(solution)/shard_map/dot_general | solution.py:36
  40.9 5.6 %fusion.14 = f32[2048,1024]{0,1:T(8,128)} fusion(bf16[1024,1,512]{2,1,0:T(2,128)(2,1)S(1)} %get-tuple-element.27, bf16[512,1024]{1,0:T(8,128)(2,1)S(1)} %get-tuple-element.39, bf16[512,1024]{1,0:T(8,128)(2,1)S(1)} %get-tuple-element.38), kind=kOutput, calls=%fused_computation.36 | convolution fusion | flops 2151677952 | bytes 11534336 | tf_op jit(solution)/shard_map/dot_general | solution.py:36
  46.5 6.6 %fusion.31 = (f32[2,128,1024]{2,1,0:T(8,128)S(1)}, f32[2,4,128,1024]{3,2,1,0:T(8,128)S(1)}, f32[2,128,1024]{2,1,0:T(8,128)}, f32[2,4,128,1024]{3,2,1,0:T(8,128)S(1)}) fusion(f32[2,4,128,2048]{3,2,1,0:T(8,128)S(1)} %bitcast.46, f32[2,4,128,2048]{3,2,1,0:T(8,128)} %bitcast.47), kind=kLoop, calls=%fused_computation.65 | loop fusion | flops 7864320 | bytes 27262976 | tf_op jit(solution)/shard_map/reduce_sum | solution.py:45
  56.0 5.5 %fusion.27 = (f32[2,128,1024]{2,1,0:T(8,128)S(1)}, f32[2,4,128,1024]{3,2,1,0:T(8,128)S(1)}, f32[2,128,1024]{2,1,0:T(8,128)S(1)}, f32[2,4,128,1024]{3,2,1,0:T(8,128)S(1)}) fusion(f32[2,4,128,2048]{3,2,1,0:T(8,128)S(1)} %bitcast.44, f32[2,4,128,2048]{3,2,1,0:T(8,128)} %bitcast.45), kind=kLoop, calls=%fused_computation.63 | loop fusion | flops 7864320 | bytes 27262976 | tf_op jit(solution)/shard_map/reduce_sum | solution.py:45
  65.5 3.6 %broadcast_multiply_fusion.2 = (f32[2,128,1024]{2,1,0:T(8,128)}, f32[2,128,1024]{2,1,0:T(8,128)S(1)}, f32[2,128,1024]{2,1,0:T(8,128)}, f32[2,128,1024]{2,1,0:T(8...) fusion(f32[2,128,1024]{2,1,0:T(8,128)S(1)} %get-tuple-element.16, ...), kind=kLoop, calls=%fused_computation.58 | loop fusion | flops 5505022 | bytes 14682120 | tf_op jit(solution)/shard_map/div | solution.py:46
  69.1 1.3 copy.21
  70.4 7.3 %all-to-all-start = ((f32[2,128,1024]{1,0,2:T(2,128)}), f32[2,128,1024]{1,0,2:T(2,128)S(1)}, u32[]{:S(2)}, u32[]{:S(2)}) async-start(f32[2,128,1024]{1,0,2:T(2,128)} %copy.21), calls=%async_computation | async-start | bytes 2097152 | tf_op jit(solution)/shard_map/all_to_all | solution.py:66
  79.0 24.5 %all-to-all-done = f32[2,128,1024]{1,0,2:T(2,128)S(1)} async-done(((f32[2,128,1024]{1,0,2:T(2,128)}), f32[2,128,1024]{1,0,2:T(2,128)S(1)}, u32[]{:S(2)}, u32[]{:S(2)}) %all-to-all-start) | async-done | bytes 1048608 | tf_op jit(solution)/shard_map/all_to_all | solution.py:66
  103.4 3.8 %all-to-all-start.1 = ((f32[2,128,1024]{1,0,2:T(2,128)}), f32[2,128,1024]{1,0,2:T(2,128)S(1)}, u32[]{:S(2)}, u32[]{:S(2)}) async-start(f32[2,128,1024]{1,0,2:T(2,128)} %copy.24), calls=%async_computation.1 | async-start | bytes 2097152 | tf_op jit(solution)/shard_map/all_to_all | solution.py:67
  107.2 3.4 %multiply_reduce_fusion = f32[2,128,1024]{2,1,0:T(8,128)S(1)} fusion(f32[2,4,128,1024]{3,2,1,0:T(8,128)} %copy-done.2, f32[2,128,1024]{2,1,0:T(8,128)} %get-tuple-element.34), kind=kLoop, calls=%fused_computation.16 | loop fusion | flops 2883584 | bytes 6291456 | tf_op jit(solution)/shard_map/reduce_sum | solution.py:47
  112.0 1.5 copy-done.6
  114.5 1.5 copy-done.4
  117.3 1.3 copy.27
  118.6 14.4 %all-to-all-done.1 = f32[2,128,1024]{1,0,2:T(2,128)S(1)} async-done(((f32[2,128,1024]{1,0,2:T(2,128)}), f32[2,128,1024]{1,0,2:T(2,128)S(1)}, u32[]{:S(2)}, u32[]{:S(2)}) %all-to-all-start.1) | async-done | bytes 1048608 | tf_op jit(solution)/shard_map/all_to_all | solution.py:67
  133.0 4.2 %all-to-all-start.2 = ((f32[2,128,1024]{1,0,2:T(2,128)}), f32[2,128,1024]{1,0,2:T(2,128)}, u32[]{:S(2)}, u32[]{:S(2)}) async-start(f32[2,128,1024]{1,0,2:T(2,128)} %copy.27), calls=%async_computation.2 | async-start | bytes 2097152 | tf_op jit(solution)/shard_map/all_to_all | solution.py:68
  137.3 6.9 %all-reduce.2 = (f32[]{:T(128)}, f32[]{:T(128)}) all-reduce(f32[]{:T(128)} %get-tuple-element.36, f32[]{:T(128)} %get-tuple-element.35), channel_id=1, replica_groups=mesh['scan'=4,'ascan'=8] {'scan'}, use_global_device_ids=true, to_apply=%region_5.6 | all-reduce | flops 2 | bytes 16 | tf_op jit(solution)/shard_map/psum | solution.py:63
  144.2 25.0 %all-reduce.1 = (f32[]{:T(128)}, f32[]{:T(128)}) all-reduce(f32[]{:T(128)} %get-tuple-element.14, f32[]{:T(128)} %get-tuple-element.15), channel_id=1, replica_groups=mesh['scan'=4,'ascan'=8] {'ascan'}, use_global_device_ids=true, to_apply=%region_6.7 | all-reduce | flops 2 | bytes 16 | tf_op jit(solution)/shard_map/psum | solution.py:63
  171.6 1.6 copy.23
  173.4 1.3 copy.30
  (44 shorter events, 17.7 us)
Async XLA Ops:
  53.1 2.0 %copy-start = (f32[2,4,128,1024]{3,2,1,0:T(8,128)}, f32[2,4,128,1024]{3,2,1,0:T(8,128)S(1)}, u32[]{:S(2)}) copy-start(f32[2,4,128,1024]{3,2,1,0:T(8,128)S(1)} %get-tuple-element.21) | copy-start | bytes 12582916
  53.1 8.4 %copy-start.2 = (f32[2,4,128,1024]{3,2,1,0:T(8,128)}, f32[2,4,128,1024]{3,2,1,0:T(8,128)S(1)}, u32[]{:S(2)}) copy-start(f32[2,4,128,1024]{3,2,1,0:T(8,128)S(1)} %get-tuple-element.43) | copy-start | bytes 12582916
  61.5 1.9 %copy-start.3 = (f32[2,4,128,1024]{3,2,1,0:T(8,128)}, f32[2,4,128,1024]{3,2,1,0:T(8,128)S(1)}, u32[]{:S(2)}) copy-start(f32[2,4,128,1024]{3,2,1,0:T(8,128)S(1)} %get-tuple-element.17) | copy-start | bytes 12582916
  61.5 7.6 %copy-start.5 = (f32[2,4,128,1024]{3,2,1,0:T(8,128)}, f32[2,4,128,1024]{3,2,1,0:T(8,128)S(1)}, u32[]{:S(2)}) copy-start(f32[2,4,128,1024]{3,2,1,0:T(8,128)S(1)} %get-tuple-element.41) | copy-start | bytes 12582916
  63.4 0.9 copy-start.11
  63.4 0.9 copy-start.12
  63.4 2.1 %copy-start.10 = (f32[2,128,1024]{2,1,0:T(8,128)S(1)}, f32[2,128,1024]{2,1,0:T(8,128)}, u32[]{:S(2)}) copy-start(f32[2,128,1024]{2,1,0:T(8,128)} %get-tuple-element.42) | copy-start | bytes 3145732
  70.4 33.0 %all-to-all-start = ((f32[2,128,1024]{1,0,2:T(2,128)}), f32[2,128,1024]{1,0,2:T(2,128)S(1)}, u32[]{:S(2)}, u32[]{:S(2)}) async-start(f32[2,128,1024]{1,0,2:T(2,128)} %copy.21), calls=%async_computation | async-start | bytes 2097152 | tf_op jit(solution)/shard_map/all_to_all | solution.py:66
  103.4 29.6 %all-to-all-start.1 = ((f32[2,128,1024]{1,0,2:T(2,128)}), f32[2,128,1024]{1,0,2:T(2,128)S(1)}, u32[]{:S(2)}, u32[]{:S(2)}) async-start(f32[2,128,1024]{1,0,2:T(2,128)} %copy.24), calls=%async_computation.1 | async-start | bytes 2097152 | tf_op jit(solution)/shard_map/all_to_all | solution.py:67
  107.2 3.8 %copy-start.1 = (f32[2,4,128,1024]{3,2,1,0:T(8,128)S(1)}, f32[2,4,128,1024]{3,2,1,0:T(8,128)}, u32[]{:S(2)}) copy-start(f32[2,4,128,1024]{3,2,1,0:T(8,128)} %copy-done) | copy-start | bytes 12582916
  107.2 4.0 %copy-start.9 = (f32[2,128,1024]{2,1,0:T(8,128)S(1)}, f32[2,128,1024]{2,1,0:T(8,128)}, u32[]{:S(2)}) copy-start(f32[2,128,1024]{2,1,0:T(8,128)} %get-tuple-element.33) | copy-start | bytes 3145732
  111.3 2.2 %copy-start.6 = (f32[2,4,128,1024]{3,2,1,0:T(8,128)S(1)}, f32[2,4,128,1024]{3,2,1,0:T(8,128)}, u32[]{:S(2)}) copy-start(f32[2,4,128,1024]{3,2,1,0:T(8,128)} %copy-done.5) | copy-start | bytes 12582916
  111.3 2.5 %copy-start.8 = (f32[2,128,1024]{2,1,0:T(8,128)S(1)}, f32[2,128,1024]{2,1,0:T(8,128)}, u32[]{:S(2)}) copy-start(f32[2,128,1024]{2,1,0:T(8,128)} %get-tuple-element.32) | copy-start | bytes 3145732
  113.8 2.2 %copy-start.4 = (f32[2,4,128,1024]{3,2,1,0:T(8,128)S(1)}, f32[2,4,128,1024]{3,2,1,0:T(8,128)}, u32[]{:S(2)}) copy-start(f32[2,4,128,1024]{3,2,1,0:T(8,128)} %copy-done.3) | copy-start | bytes 12582916
  113.8 2.5 %copy-start.7 = (f32[2,128,1024]{2,1,0:T(8,128)S(1)}, f32[2,128,1024]{2,1,0:T(8,128)}, u32[]{:S(2)}) copy-start(f32[2,128,1024]{2,1,0:T(8,128)} %get-tuple-element.30) | copy-start | bytes 3145732
  133.0 43.4 %all-to-all-start.2 = ((f32[2,128,1024]{1,0,2:T(2,128)}), f32[2,128,1024]{1,0,2:T(2,128)}, u32[]{:S(2)}, u32[]{:S(2)}) async-start(f32[2,128,1024]{1,0,2:T(2,128)} %copy.27), calls=%async_computation.2 | async-start | bytes 2097152 | tf_op jit(solution)/shard_map/all_to_all | solution.py:68
